TPU v7x, 32 devices: a whole 2x2x4 slice. The times are simulated.
32 devices in a mesh: gx: 4 (over z), gy: 4 (over x, core), col: 2 (over y).
Axes of the slice: x: 2, y: 2, z: 4, core: 2. Of those that a mesh axis runs over, the one named last changes fastest.
Arguments:
- fields: bfloat16 [2, 128, 128, 32, 128], P('col', 'gx', 'gy'), may hold values from -6 to 6
- spectral: bfloat16 [1, 16, 16, 2, 32, 32, 16], P(None, 'gx', 'gy', None, None, 'col'), may hold values from -0.75 to 0.75
- skip_weight: bfloat16 [1, 32, 32], replicated, may hold values from -1 to 1
- skip_bias: float32 [1, 32], replicated, may hold values from -3 to 3
- norm_gain: float32 [1, 32], replicated, may hold values from 0.5 to 1.5
- norm_shift: float32 [1, 32], replicated, may hold values from -3 to 3
Outputs:
- activations: bfloat16 [2, 128, 128, 32, 128], P('col', 'gx', 'gy')
All inputs are finite; a program needn't handle non-finite values.
Results may differ from a plain program's by a relative error of at most 0.012.
Values may be sent and summed in bfloat16 or wider, within the bound.
A program may use at most 128 MiB of HBM per device.

v0:
```python
import math
import jax
import jax.numpy as jnp
from jax import lax
from jax.sharding import PartitionSpec as P

X = 128
Y = 128
Z = 128
MX = 16
MY = 16
MZ = 16
norm_eps = 1e-05


def signed_freqs(count):
    index = jnp.arange(count, dtype=jnp.int32)
    return jnp.where(index < count // 2, index, index - count)


def angles(positions, frequency, length):
    turn_count = positions[:, None] * frequency[None, :] % length
    return turn_count.astype(jnp.float32) * (2.0 * math.pi / length)


def forward_table(positions, frequency, length, factor):
    phase_angle = angles(positions, frequency, length)
    cosine = jnp.cos(phase_angle) * factor
    sine_part = jnp.sin(phase_angle) * factor
    from_real = jnp.stack([cosine, -sine_part], axis=-1)
    from_imag = jnp.stack([sine_part, cosine], axis=-1)
    return jnp.stack([from_real, from_imag], axis=1)


def inverse_table(frequency, positions, length):
    phase_angle = angles(positions, frequency, length).T
    cosine = jnp.cos(phase_angle)
    sine_part = jnp.sin(phase_angle)
    from_real = jnp.stack([cosine, sine_part], axis=-1)
    from_imag = jnp.stack([-sine_part, cosine], axis=-1)
    return jnp.stack([from_real, from_imag], axis=1)


def depth_tables(length, count):
    frequency = jnp.arange(count, dtype=jnp.int32)
    phase_angle = angles(jnp.arange(length, dtype=jnp.int32), frequency, length)
    forward = jnp.concatenate([jnp.cos(phase_angle), -jnp.sin(phase_angle)], axis=1)
    backward = jnp.concatenate([jnp.cos(phase_angle).T, -jnp.sin(phase_angle).T], axis=0)
    return (forward.astype(jnp.bfloat16), backward.astype(jnp.bfloat16))


def mix_modes(spectrum, weight):

    def contract(left, right):
        return jnp.einsum("abcz,abcdz->abdz", left, right, preferred_element_type=jnp.float32)

    real_in = spectrum[:, :, :, 0]
    imag_in = spectrum[:, :, :, 1]
    real_weight = weight[:, :, 0]
    imag_weight = weight[:, :, 1]
    real_out = contract(real_in, real_weight) - contract(imag_in, imag_weight)
    imag_out = contract(real_in, imag_weight) + contract(imag_in, real_weight)
    return jnp.stack([real_out, imag_out], axis=3)


def finish(spectral_part, skip_part, offset, scaling, shift_term):
    pre_norm = spectral_part + skip_part + offset[:, None]
    centre = jnp.mean(pre_norm, axis=2, keepdims=True)
    spread = jnp.mean(jnp.square(pre_norm - centre), axis=2, keepdims=True)
    normed = (pre_norm - centre) * lax.rsqrt(spread + norm_eps) * scaling[:, None] + shift_term[
        :, None
    ]
    return jax.nn.gelu(normed, approximate=False).astype(jnp.bfloat16)


def local(fields, spectral, skip_weight, skip_bias, norm_gain, norm_shift):
    highest = lax.Precision.HIGHEST
    hidden = fields[0]
    tile_first, tile_second, channels, depth_cells = hidden.shape
    first_cells = lax.axis_index("gx") * tile_first + jnp.arange(tile_first, dtype=jnp.int32)
    second_cells = lax.axis_index("gy") * tile_second + jnp.arange(tile_second, dtype=jnp.int32)
    depth_forward, depth_backward = depth_tables(Z, MZ)
    second_forward = forward_table(second_cells, signed_freqs(MY), Y, 1.0).astype(jnp.bfloat16)
    first_forward = forward_table(first_cells, signed_freqs(MX), X, 1.0 / math.sqrt(X * Y * Z))
    first_inverse = inverse_table(signed_freqs(MX), first_cells, X).astype(jnp.bfloat16)
    second_inverse = inverse_table(signed_freqs(MY), second_cells, Y)
    inverse_scale = 1.0 / math.sqrt(MX * MY * MZ)
    amplitude = jnp.dot(
        hidden.reshape(-1, depth_cells), depth_forward, preferred_element_type=jnp.float32
    )
    amplitude = amplitude.astype(jnp.bfloat16).reshape(tile_first, tile_second, channels, 2, MZ)
    along_second = jnp.einsum(
        "xycrz,yrks->xkcsz", amplitude, second_forward, preferred_element_type=jnp.float32
    )
    summed_second = lax.psum_scatter(
        along_second.astype(jnp.bfloat16), "gy", scatter_dimension=1, tiled=True
    ).astype(jnp.float32)
    partial_modes = jnp.einsum("xkcsz,xsjt->jkctz", summed_second, first_forward, precision=highest)
    summed = lax.psum_scatter(
        partial_modes.astype(jnp.bfloat16), "gx", scatter_dimension=0, tiled=True
    )
    weights_here = spectral[0]
    mixed_modes = mix_modes(summed, lax.all_gather(weights_here, "col", axis=4, tiled=True)).astype(
        jnp.bfloat16
    )
    gathered_second = lax.all_gather(mixed_modes, "gy", axis=1, tiled=True)
    full_modes = lax.all_gather(gathered_second, "gx", axis=0, tiled=True)
    rows_first = jnp.einsum(
        "jkcsz,jsxt->xkctz", full_modes, first_inverse, preferred_element_type=jnp.float32
    )
    rows_both = jnp.einsum(
        "xkcsz,ksyt->xyctz", rows_first, second_inverse, precision=highest
    ).astype(jnp.bfloat16)
    spectral_part = jnp.dot(
        rows_both.reshape(-1, 2 * MZ), depth_backward, preferred_element_type=jnp.float32
    )
    spectral_part = (
        spectral_part.reshape(tile_first, tile_second, channels, depth_cells) * inverse_scale
    )
    skip_part = jnp.einsum(
        "oc,xycz->xyoz", skip_weight[0], hidden, preferred_element_type=jnp.float32
    )
    hidden = finish(spectral_part, skip_part, skip_bias[0], norm_gain[0], norm_shift[0])
    return hidden[None]


def solution(mesh):
    placed = (
        P("col", "gx", "gy", None, None),
        P(None, "gx", "gy", None, None, "col", None),
        P(),
        P(),
        P(),
        P(),
    )
    return jax.shard_map(
        local,
        mesh=mesh,
        in_specs=placed,
        out_specs=P("col", "gx", "gy", None, None),
        check_vma=False,
    )
```

profile of v0, /device:TPU:0, one launch (start us, length us, event | category | flops | bytes accessed | tf_op | source)
XLA Modules:
  0.0 268.1 jit_solution(5952482807343169716)
XLA Ops:
  7.4 6.4 %fusion = bf16[32768,32]{0,1:T(8,128)(2,1)S(1)} fusion(bf16[32768,128]{1,0:T(8,128)(2,1)} %bitcast.159, bf16[128,16]{0,1:T(8,128)(2,1)S(1)} %get-tuple-element.37, bf16[128,16]{0,1:T(8,128)(2,1)S(1)} %get-tuple-element.38), kind=kOutput, calls=%fused_computation.1 | convolution fusion | flops 269500416 | bytes 10493952 | tf_op jit(solution)/shard_map/dot_general | solution.py:88
  13.8 7.9 %reshape.722 = bf16[32,32,32,2,16]{2,1,0,4,3:T(8,128)(2,1)} reshape(bf16[32768,32]{0,1:T(8,128)(2,1)S(1)} %fusion) | data formatting | bytes 4194304 | tf_op jit(solution)/shard_map/reshape | solution.py:91
  21.9 4.7 %fusion.24 = bf16[32,16,32,2,16]{2,1,4,0,3:T(8,128)(2,1)S(1)} fusion(bf16[32,32,32,2,16]{2,1,0,4,3:T(8,128)(2,1)} %reshape.722, bf16[32,1,16,2]{0,2,1,3:T(8,128)(2,1)S(1)} %get-tuple-element.16, bf16[32,1,16,2]{0,2,1,3:T(8,128)(2,1)S(1)} %get-tuple-element.15), kind=kOutput, calls=%fused_computation.37 | convolution fusion | flops 67641344 | bytes 3149824 | tf_op jit(solution)/shard_map/xycrz,yrks->xkcsz/dot_general | solution.py:92
  26.6 3.1 %copy.26 = bf16[32,16,32,2,16]{2,4,3,0,1:T(8,128)(2,1)} copy(bf16[32,16,32,2,16]{2,1,4,0,3:T(8,128)(2,1)S(1)} %fusion.24) | data formatting | bytes 2097152 | tf_op jit(solution)/shard_map/convert_element_type | solution.py:96
  30.8 15.1 %fusion.13 = f32[32,32,128,32]{2,3,1,0:T(8,128)} fusion(bf16[1,32,32,32,128]{4,3,2,1,0:T(8,128)(2,1)} %param.6, bf16[1,32,32]{2,1,0:T(8,128)(2,1)S(1)} %copy-done), kind=kOutput, calls=%fused_computation.27 | convolution fusion | flops 268435456 | bytes 25167872 | tf_op jit(solution)/shard_map/oc,xycz->xyoz/dot_general | solution.py:120
  46.0 31.2 %reduce-scatter.3.cloned.1.call-done = bf16[32,4,32,2,16]{2,4,3,0,1:T(8,128)(2,1)} async-done(((bf16[32,16,32,2,16]{2,4,3,0,1:T(8,128)(2,1)}), bf16[32,4,32,2,16]{2,4,3,0,1:T(8,128)(2,1)}) %reduce-scatter.3.cloned.1.call-update) | async-done | bytes 262160 | tf_op jit(solution)/shard_map/reduce_scatter | solution.py:95
  77.2 1.9 fusion.30
  79.1 0.9 copy.29
  80.1 11.0 %all-gather.3.cloned.1.call-done = bf16[1,4,4,2,32,32,16]{4,6,5,3,2,1,0:T(8,128)(2,1)} async-done(((bf16[1,4,4,2,32,16,16]{4,6,5,3,2,1,0:T(8,128)(2,1)}), bf16[1,4,4,2,32,32,16]{4,6,5,3,2,1,0:T(8,128)(2,1)}) %all-gather.3.cloned.1.call-update) | async-done | bytes 1048592 | tf_op jit(solution)/shard_map/all_gather | solution.py:103
  91.1 4.5 %slice_bitcast_fusion = (bf16[4,4,32,32,16]{2,4,3,1,0:T(8,128)(2,1)}, bf16[4,4,32,32,16]{2,4,3,1,0:T(8,128)(2,1)S(1)}) fusion(bf16[4,4,2,32,32,16]{3,5,4,2,1,0:T(8,128)(2,1)} %bitcast.161), kind=kLoop, calls=%fused_computation.39 | loop fusion | bytes 2097152 | tf_op jit(solution)/shard_map/squeeze | solution.py:60
  95.6 4.5 %copy.44 = bf16[4,4,32,32,16]{3,2,4,1,0:T(8,128)(2,1)} copy(bf16[4,4,32,32,16]{2,4,3,1,0:T(8,128)(2,1)} %get-tuple-element.5) | data formatting | bytes 1048576 | tf_op jit(solution)/shard_map/squeeze | solution.py:60
  100.2 2.9 %copy.41 = bf16[4,4,32,32,16]{3,2,4,1,0:T(8,128)(2,1)} copy(bf16[4,4,32,32,16]{2,4,3,1,0:T(8,128)(2,1)S(1)} %get-tuple-element.6) | data formatting | bytes 1048576 | tf_op jit(solution)/shard_map/squeeze | solution.py:59
  104.0 2.2 fusion.39
  106.2 2.3 fusion.37
  108.5 2.3 fusion.35
  110.7 2.2 fusion.41
  113.1 7.2 %all_gather.10 = bf16[4,16,32,2,16]{2,4,3,0,1:T(8,128)(2,1)S(1)} all-gather(bf16[4,4,32,2,16]{2,4,3,0,1:T(8,128)(2,1)S(1)} %pad_maximum_fusion), channel_id=1, replica_groups=mesh['gx'=4,'gy'=4,'col'=2] {'gy'}, dimensions={1}, use_global_device_ids=true | all-gather | bytes 163840 | tf_op jit(solution)/shard_map/all_gather | solution.py:106
  120.3 38.6 %all_gather.11 = bf16[16,16,32,2,16]{2,4,3,1,0:T(8,128)(2,1)S(1)} all-gather(bf16[4,16,32,2,16]{2,4,3,1,0:T(8,128)(2,1)S(1)} %copy.30), channel_id=1, replica_groups=mesh['gx'=4,'gy'=4,'col'=2] {'gx'}, dimensions={0}, use_global_device_ids=true | all-gather | bytes 655360 | tf_op jit(solution)/shard_map/all_gather | solution.py:107
  158.8 1.5 convolution_bitcast_fusion
  160.3 22.8 %fusion.12 = bf16[32,32,32,2,16]{2,1,4,0,3:T(8,128)(2,1)} fusion(f32[32,16,32,2,16]{2,0,4,1,3:T(8,128)S(1)} %convolution_bitcast_fusion, f32[16,1,32,2]{2,0,3,1:T(8,128)S(1)} %get-tuple-element.10, f32[16,1,32,2]{2,0,3,1:T(8,128)S(1)} %get-tuple-element.9), kind=kOutput, calls=%fused_computation.26 | convolution fusion | flops 403703808 | bytes 4202496 | tf_op jit(solution)/shard_map/xkcsz,ksyt->xyctz/dot_general | solution.py:111
  183.1 10.5 %copy.34 = bf16[32,32,32,2,16]{2,4,3,1,0:T(8,128)(2,1)} copy(bf16[32,32,32,2,16]{2,1,4,0,3:T(8,128)(2,1)} %fusion.12) | data formatting | bytes 4194304 | tf_op jit(solution)/shard_map/convert_element_type | solution.py:113
  193.6 14.5 %fusion.93 = (f32[32,32,128]{2,1,0:T(8,128)S(1)}, f32[32,32,32,128]{3,2,1,0:T(8,128)}) fusion(f32[32]{0:T(128)S(1)} %bitcast.164, f32[32,32,128,32]{2,3,1,0:T(8,128)} %fusion.13, bf16[32,32,32,32]{2,3,1,0:T(8,128)(2,1)} %bitcast.160, bf16[16,128]{1,0:T(8,128)(2,1)S(1)} %get-tuple-element.41, bf16[16,128]{1,0:T(8,128)(2,1)S(1)} %get-tuple-element.42), kind=kOutput, calls=%fused_computation.167 | convolution fusion | flops 285097984 | bytes 36184192 | tf_op jit(solution)/shard_map/dot_general | solution.py:114
  208.2 10.9 %multiply_reduce_fusion = f32[32,32,128]{2,1,0:T(8,128)S(1)} fusion(f32[32,32,32,128]{3,2,1,0:T(8,128)} %get-tuple-element.36, f32[32,32,128]{2,1,0:T(8,128)S(1)} %broadcast_multiply_fusion), kind=kLoop, calls=%fused_computation.23 | loop fusion | flops 12451840 | bytes 17825792 | tf_op jit(solution)/shard_map/reduce_sum | solution.py:69
  219.2 41.4 %fusion.21 = bf16[1,32,32,32,128]{4,3,2,1,0:T(8,128)(2,1)} fusion(f32[32]{0:T(128)S(1)} %bitcast.162, f32[32]{0:T(128)S(1)} %bitcast.163, f32[32,32,128]{2,1,0:T(8,128)S(1)} %add_rsqrt_fusion, f32[32,32,32,128]{3,2,1,0:T(8,128)} %get-tuple-element.36, f32[32,32,128]{2,1,0:T(8,128)S(1)} %broadcast_multiply_fusion), kind=kLoop, calls=%fused_computation.36 | loop fusion | flops 289406976 | bytes 26214656 | tf_op jit(solution)/shard_map/broadcast_in_dim | solution.py:124
  (34 shorter events, 2.4 us)
Async XLA Ops:
  7.4 23.4 %copy-start = (bf16[1,32,32]{2,1,0:T(8,128)(2,1)S(1)}, bf16[1,32,32]{2,1,0:T(8,128)(2,1)}, u32[]{:S(2)}) copy-start(bf16[1,32,32]{2,1,0:T(8,128)(2,1)} %param.8) | copy-start | bytes 6148
  7.4 69.8 %reduce-scatter.3.cloned.1.call-start = ((), (), s32[]{:S(2)}) async-start(), calls=%async_computation.2 | async-start | bytes 5242880 | tf_op jit(solution)/shard_map/reduce_scatter | solution.py:95
  29.7 61.4 %all-gather.3.cloned.1.call-start = ((), (), s32[]{:S(2)}) async-start(), calls=%async_computation.4 | async-start | bytes 6291456 | tf_op jit(solution)/shard_map/all_gather | solution.py:103
  30.3 72.8 %reduce-scatter.5.cloned.1.call-start = ((), (), s32[]{:S(2)}) async-start(), calls=%async_computation.3 | async-start | bytes 655360 | tf_op jit(solution)/shard_map/reduce_scatter | solution.py:99
  160.3 33.3 %copy-start.4 = (f32[1,32]{1,0:T(1,128)S(1)}, f32[1,32]{1,0:T(1,128)}, u32[]{:S(2)}) copy-start(f32[1,32]{1,0:T(1,128)} %param.9) | copy-start | bytes 388
  208.1 11.1 %copy-start.2 = (f32[1,32]{1,0:T(1,128)S(1)}, f32[1,32]{1,0:T(1,128)}, u32[]{:S(2)}) copy-start(f32[1,32]{1,0:T(1,128)} %param.11) | copy-start | bytes 388
  208.1 11.1 %copy-start.3 = (f32[1,32]{1,0:T(1,128)S(1)}, f32[1,32]{1,0:T(1,128)}, u32[]{:S(2)}) copy-start(f32[1,32]{1,0:T(1,128)} %param.10) | copy-start | bytes 388
  208.2 52.5 %copy-start.1 = (bf16[1,32,32]{2,1,0:T(8,128)(2,1)S(1)}, bf16[1,32,32]{2,1,0:T(8,128)(2,1)}, u32[]{:S(2)}) copy-start(bf16[1,32,32]{2,1,0:T(8,128)(2,1)} %param.8) | copy-start | bytes 6148
Sparse Core Ops, SparseCore 0:
  29.9 47.2 reduce-scatter.2
  80.2 21.8 reduce-scatter.4
Sparse Core Ops, SparseCore 1:
  31.8 59.3 all-gather.2
where the time goes:
time: 269 us; the launch traced here: 268 us
  matrix products  75.9 us (28%)
  other arithmetic  53 us (20%)
  blocking collectives  45.7 us (17%)
  waiting for transfers between devices  42.8 us (16%)
  local copies, waits for them, and re-layouts  35.4 us (13%)
  between operations  15 us (6%)
    broadcast_in_dim x1, other arithmetic, local(): return hidden[None]  41.4 us
    all_gather x1, blocking collectives, local(): full_modes = lax.all_gather(gathered_second, 'gx', axis=0, tiled=True)  38.6 us
    reduce_scatter x1, waiting for transfers between devices, local(): lax.psum_scatter(along_second.astype(jnp.bfloat16), 'gy', scatter_dimensi...  31.2 us
    dot_general x1, matrix products, local(): jnp.einsum('xkcsz,ksyt->xyctz', rows_first, second_inverse, precision=hig...  22.8 us
    dot_general x1, matrix products, local(): jnp.einsum('oc,xycz->xyoz', skip_weight[0], hidden, preferred_element_typ...  15.1 us
    dot_general x1, matrix products, local(): jnp.dot(rows_both.reshape(-1, 2 * MZ), depth_backward, preferred_element_...  14.5 us
    all_gather x1, waiting for transfers between devices, local(): lax.all_gather(weights_here, 'col', axis=4, tiled=True)  11 us
    reduce_sum x1, other arithmetic, finish(): spread = jnp.mean(jnp.square(pre_norm - centre), axis=2, keepdims=True)  10.9 us
  transfers between devices with their start and end apart: 3, of which 2 were waited for; matrix products, arithmetic and copies ran while one was open for 11% of the time, Pallas kernels for 0%

commit v1 on v0

--- a/solution.py
+++ b/solution.py
@@ -104,10 +104,22 @@
         jnp.bfloat16
     )
     gathered_second = lax.all_gather(mixed_modes, "gy", axis=1, tiled=True)
-    full_modes = lax.all_gather(gathered_second, "gx", axis=0, tiled=True)
-    rows_first = jnp.einsum(
-        "jkcsz,jsxt->xkctz", full_modes, first_inverse, preferred_element_type=jnp.float32
-    )
+    peers, position, extent = (lax.axis_size("gx"), lax.axis_index("gx"), gathered_second.shape[0])
+    right_2 = [(i, (i + 1) % peers) for i in range(peers)]
+    block, running = (gathered_second, None)
+    for step in range(peers):
+        following = lax.ppermute(block, "gx", right_2) if step < peers - 1 else None
+        take_in = jnp.einsum(
+            "jkcsz,jsxt->xkctz",
+            block,
+            lax.dynamic_slice_in_dim(
+                first_inverse, (position - step) % peers * extent, block.shape[0], axis=0
+            ),
+            preferred_element_type=jnp.float32,
+        )
+        running = take_in if running is None else running + take_in
+        block = following
+    rows_first = running
     rows_both = jnp.einsum(
         "xkcsz,ksyt->xyctz", rows_first, second_inverse, precision=highest
     ).astype(jnp.bfloat16)

time: 269 us -> 287 us (1.067); the launches traced: 268 us -> 282 us
  blocking collectives: 45.7 us -> 7.15 us
  waiting for transfers between devices: 42.8 us -> 75.1 us
  matrix products: 75.9 us -> 93.1 us
    all_gather x1 -> x0, blocking collectives: 38.6 us -> none  [local(): full_modes = lax.all_gather(gathered_second, 'gx', axis=0, tiled=True)]
    ppermute x0 -> x3, waiting for transfers between devices: none -> 32.8 us  [local(): following = lax.ppermute(block, 'gx', right_2) if step < peers - 1 else None]
    dot_general x1 -> x4, matrix products: 1.49 us -> 18.6 us  [local(): jnp.einsum('jkcsz,jsxt->xkctz', block, lax.dynamic_slice_in_dim(first_inv...]
  transfers between devices with their start and end apart: 3 -> 6, of which waited for: 2 -> 5; matrix products, arithmetic and copies ran while one was open for 11% -> 15% of each run, Pallas kernels for 0% -> 0%
where the time goes in v1:
time: 287 us; the launch traced here: 282 us
  matrix products  93.1 us (32%)
  waiting for transfers between devices  75.1 us (26%)
  other arithmetic  53 us (18%)
  local copies, waits for them, and re-layouts  35.7 us (12%)
  between operations  15.4 us (5%)
  blocking collectives  7.15 us (2%)
    broadcast_in_dim x1, other arithmetic, local(): return hidden[None]  41.4 us
    ppermute x3, waiting for transfers between devices, local(): following = lax.ppermute(block, 'gx', right_2) if step < peers - 1 else None  32.8 us
    reduce_scatter x1, waiting for transfers between devices, local(): lax.psum_scatter(along_second.astype(jnp.bfloat16), 'gy', scatter_dimensi...  30.7 us
    dot_general x1, matrix products, local(): jnp.einsum('xkcsz,ksyt->xyctz', rows_first, second_inverse, precision=hig...  22.8 us
    dot_general x4, matrix products, local(): jnp.einsum('jkcsz,jsxt->xkctz', block, lax.dynamic_slice_in_dim(first_inv...  18.6 us
    dot_general x1, matrix products, local(): jnp.einsum('oc,xycz->xyoz', skip_weight[0], hidden, preferred_element_typ...  15.2 us
    dot_general x1, matrix products, local(): jnp.dot(rows_both.reshape(-1, 2 * MZ), depth_backward, preferred_element_...  14.4 us
    all_gather x1, waiting for transfers between devices, local(): lax.all_gather(weights_here, 'col', axis=4, tiled=True)  11 us
  transfers between devices with their start and end apart: 6, of which 5 were waited for; matrix products, arithmetic and copies ran while one was open for 15% of the time, Pallas kernels for 0%

profile of v1, /device:TPU:0, one launch (start us, length us, event | category | flops | bytes accessed | tf_op | source)
XLA Modules:
  0.0 281.6 jit_solution(13112532591744908951)
XLA Ops:
  7.4 6.4 %fusion = bf16[32768,32]{0,1:T(8,128)(2,1)S(1)} fusion(bf16[32768,128]{1,0:T(8,128)(2,1)} %bitcast.198, bf16[128,16]{0,1:T(8,128)(2,1)S(1)} %get-tuple-element.37, bf16[128,16]{0,1:T(8,128)(2,1)S(1)} %get-tuple-element.38), kind=kOutput, calls=%fused_computation.1 | convolution fusion | flops 269500416 | bytes 10493952 | tf_op jit(solution)/shard_map/dot_general | solution.py:88
  13.8 7.9 %reshape.722 = bf16[32,32,32,2,16]{2,1,0,4,3:T(8,128)(2,1)} reshape(bf16[32768,32]{0,1:T(8,128)(2,1)S(1)} %fusion) | data formatting | bytes 4194304 | tf_op jit(solution)/shard_map/reshape | solution.py:91
  21.9 4.7 %fusion.25 = bf16[32,16,32,2,16]{2,1,4,0,3:T(8,128)(2,1)S(1)} fusion(bf16[32,32,32,2,16]{2,1,0,4,3:T(8,128)(2,1)} %reshape.722, bf16[32,1,16,2]{0,2,1,3:T(8,128)(2,1)S(1)} %get-tuple-element.16, bf16[32,1,16,2]{0,2,1,3:T(8,128)(2,1)S(1)} %get-tuple-element.15), kind=kOutput, calls=%fused_computation.41 | convolution fusion | flops 67641344 | bytes 3149824 | tf_op jit(solution)/shard_map/xycrz,yrks->xkcsz/dot_general | solution.py:92
  26.6 3.1 %copy.26 = bf16[32,16,32,2,16]{2,4,3,0,1:T(8,128)(2,1)} copy(bf16[32,16,32,2,16]{2,1,4,0,3:T(8,128)(2,1)S(1)} %fusion.25) | data formatting | bytes 2097152 | tf_op jit(solution)/shard_map/convert_element_type | solution.py:96
  31.2 15.2 %fusion.13 = f32[32,32,128,32]{2,3,1,0:T(8,128)} fusion(bf16[1,32,32,32,128]{4,3,2,1,0:T(8,128)(2,1)} %param.6, bf16[1,32,32]{2,1,0:T(8,128)(2,1)S(1)} %copy-done), kind=kOutput, calls=%fused_computation.27 | convolution fusion | flops 268435456 | bytes 25167872 | tf_op jit(solution)/shard_map/oc,xycz->xyoz/dot_general | solution.py:132
  46.5 30.7 %reduce-scatter.3.cloned.1.call-done = bf16[32,4,32,2,16]{2,4,3,0,1:T(8,128)(2,1)} async-done(((bf16[32,16,32,2,16]{2,4,3,0,1:T(8,128)(2,1)}), bf16[32,4,32,2,16]{2,4,3,0,1:T(8,128)(2,1)}) %reduce-scatter.3.cloned.1.call-update) | async-done | bytes 262160 | tf_op jit(solution)/shard_map/reduce_scatter | solution.py:95
  80.1 11.0 %all-gather.3.cloned.1.call-done = bf16[1,4,4,2,32,32,16]{4,6,5,3,2,1,0:T(8,128)(2,1)} async-done(((bf16[1,4,4,2,32,16,16]{4,6,5,3,2,1,0:T(8,128)(2,1)}), bf16[1,4,4,2,32,32,16]{4,6,5,3,2,1,0:T(8,128)(2,1)}) %all-gather.3.cloned.1.call-update) | async-done | bytes 1048592 | tf_op jit(solution)/shard_map/all_gather | solution.py:103
  91.1 4.5 %slice_bitcast_fusion = (bf16[4,4,32,32,16]{2,4,3,1,0:T(8,128)(2,1)}, bf16[4,4,32,32,16]{2,4,3,1,0:T(8,128)(2,1)S(1)}) fusion(bf16[4,4,2,32,32,16]{3,5,4,2,1,0:T(8,128)(2,1)} %bitcast.200), kind=kLoop, calls=%fused_computation.42 | loop fusion | bytes 2097152 | tf_op jit(solution)/shard_map/squeeze | solution.py:60
  95.6 4.5 %copy.44 = bf16[4,4,32,32,16]{3,2,4,1,0:T(8,128)(2,1)} copy(bf16[4,4,32,32,16]{2,4,3,1,0:T(8,128)(2,1)} %get-tuple-element.5) | data formatting | bytes 1048576 | tf_op jit(solution)/shard_map/squeeze | solution.py:60
  100.2 2.9 %copy.41 = bf16[4,4,32,32,16]{3,2,4,1,0:T(8,128)(2,1)} copy(bf16[4,4,32,32,16]{2,4,3,1,0:T(8,128)(2,1)S(1)} %get-tuple-element.6) | data formatting | bytes 1048576 | tf_op jit(solution)/shard_map/squeeze | solution.py:59
  108.5 2.3 fusion.47
  110.7 2.3 fusion.45
  113.1 7.2 %all_gather.7 = bf16[4,16,32,2,16]{2,4,3,0,1:T(8,128)(2,1)S(1)} all-gather(bf16[4,4,32,2,16]{2,4,3,0,1:T(8,128)(2,1)S(1)} %pad_maximum_fusion), channel_id=1, replica_groups=mesh['gx'=4,'gy'=4,'col'=2] {'gy'}, dimensions={1}, use_global_device_ids=true | all-gather | bytes 163840 | tf_op jit(solution)/shard_map/all_gather | solution.py:106
  123.5 13.0 %collective-permute-done = bf16[4,16,32,2,16]{2,0,3,4,1:T(4,128)(2,1)S(1)} collective-permute-done((bf16[4,16,32,2,16]{2,0,3,4,1:T(4,128)(2,1)S(1)}, bf16[4,16,32,2,16]{2,0,3,4,1:T(4,128)(2,1)S(1)}, u32[]{:S(2)}, u32[]{:S(2)}) %collective-permute-start) | collective-permute-done | bytes 131104 | tf_op jit(solution)/shard_map/ppermute | solution.py:111
  136.5 4.7 %fusion.35 = f32[32,2,16,32,16,1]{3,0,5,4,2,1:T(8,128)} fusion(bf16[4,16,32,2,16]{2,0,3,4,1:T(4,128)(2,1)S(1)} %collective-permute-done, s32[]{:T(128)S(6)} %select_n.151, bf16[16,1,32,2]{2,0,1,3:T(8,128)(2,1)S(1)} %get-tuple-element.14, bf16[16,1,32,2]{2,0,1,3:T(8,128)(2,1)S(1)} %get-tuple-element.13), kind=kOutput, calls=%fused_computation.52 | convolution fusion | flops 8390656 | bytes 2232324 | tf_op jit(solution)/shard_map/jkcsz,jsxt->xkctz/dot_general | solution.py:112
  141.3 10.4 %collective-permute-done.1 = bf16[4,16,32,2,16]{2,0,3,4,1:T(4,128)(2,1)S(1)} collective-permute-done((bf16[4,16,32,2,16]{2,0,3,4,1:T(4,128)(2,1)S(1)}, bf16[4,16,32,2,16]{2,0,3,4,1:T(4,128)(2,1)S(1)}, u32[]{:S(2)}, u32[]{:S(2)}) %collective-permute-start.1) | collective-permute-done | bytes 131104 | tf_op jit(solution)/shard_map/ppermute | solution.py:111
  151.8 4.9 %fusion.33 = f32[32,2,16,32,16,1]{3,0,5,4,2,1:T(8,128)} fusion(bf16[4,16,32,2,16]{2,0,3,4,1:T(4,128)(2,1)S(1)} %collective-permute-done.1, s32[]{:T(128)S(6)} %select_n.153, bf16[16,1,32,2]{2,0,1,3:T(8,128)(2,1)S(1)} %get-tuple-element.14, bf16[16,1,32,2]{2,0,1,3:T(8,128)(2,1)S(1)} %get-tuple-element.13), kind=kOutput, calls=%fused_computation.50 | convolution fusion | flops 8390656 | bytes 2232324 | tf_op jit(solution)/shard_map/jkcsz,jsxt->xkctz/dot_general | solution.py:112
  156.7 9.4 %collective-permute-done.2 = bf16[4,16,32,2,16]{2,0,3,4,1:T(4,128)(2,1)S(1)} collective-permute-done((bf16[4,16,32,2,16]{2,0,3,4,1:T(4,128)(2,1)S(1)}, bf16[4,16,32,2,16]{2,0,3,4,1:T(4,128)(2,1)S(1)}, u32[]{:S(2)}, u32[]{:S(2)}) %collective-permute-start.2) | collective-permute-done | bytes 131104 | tf_op jit(solution)/shard_map/ppermute | solution.py:111
  166.1 7.6 %fusion.17 = f32[32,16,32,2,16]{2,0,4,1,3:T(8,128)S(1)} fusion(f32[32,2,16,32,16,1]{3,0,5,4,2,1:T(8,128)} %fusion.33, f32[32,2,16,32,16,1]{3,0,5,4,2,1:T(8,128)} %fusion.35, f32[32,2,16,32,16,1]{3,0,5,4,2,1:T(8,128)S(1)} %fusion.37, bf16[4,16,32,2,16]{2,0,3,4,1:T(4,128)(2,1)S(1)} %collective-permute-done.2, s32[]{:T(128)S(6)} %select_n.155, ...), kind=kOutput, calls=%fused_computation.32 | convolution fusion | flops 9963520 | bytes 8523780 | tf_op jit(solution)/shard_map/jkcsz,jsxt->xkctz/dot_general | solution.py:112
  173.7 22.8 %fusion.12 = bf16[32,32,32,2,16]{2,1,4,0,3:T(8,128)(2,1)} fusion(f32[32,16,32,2,16]{2,0,4,1,3:T(8,128)S(1)} %fusion.17, f32[16,1,32,2]{2,0,3,1:T(8,128)S(1)} %get-tuple-element.10, f32[16,1,32,2]{2,0,3,1:T(8,128)S(1)} %get-tuple-element.9), kind=kOutput, calls=%fused_computation.26 | convolution fusion | flops 403703808 | bytes 4202496 | tf_op jit(solution)/shard_map/xkcsz,ksyt->xyctz/dot_general | solution.py:123
  196.4 10.5 %copy.34 = bf16[32,32,32,2,16]{2,4,3,1,0:T(8,128)(2,1)} copy(bf16[32,32,32,2,16]{2,1,4,0,3:T(8,128)(2,1)} %fusion.12) | data formatting | bytes 4194304 | tf_op jit(solution)/shard_map/convert_element_type | solution.py:125
  207.0 14.4 %fusion.117 = (f32[32,32,128]{2,1,0:T(8,128)S(1)}, f32[32,32,32,128]{3,2,1,0:T(8,128)}) fusion(f32[32]{0:T(128)S(1)} %bitcast.203, f32[32,32,128,32]{2,3,1,0:T(8,128)} %fusion.13, bf16[32,32,32,32]{2,3,1,0:T(8,128)(2,1)} %bitcast.199, bf16[16,128]{1,0:T(8,128)(2,1)S(1)} %get-tuple-element.41, bf16[16,128]{1,0:T(8,128)(2,1)S(1)} %get-tuple-element.42), kind=kOutput, calls=%fused_computation.196 | convolution fusion | flops 285097984 | bytes 36184192 | tf_op jit(solution)/shard_map/dot_general | solution.py:126
  221.5 10.9 %multiply_reduce_fusion = f32[32,32,128]{2,1,0:T(8,128)S(1)} fusion(f32[32,32,32,128]{3,2,1,0:T(8,128)} %get-tuple-element.36, f32[32,32,128]{2,1,0:T(8,128)S(1)} %broadcast_multiply_fusion), kind=kLoop, calls=%fused_computation.23 | loop fusion | flops 12451840 | bytes 17825792 | tf_op jit(solution)/shard_map/reduce_sum | solution.py:69
  232.5 41.4 %fusion.22 = bf16[1,32,32,32,128]{4,3,2,1,0:T(8,128)(2,1)} fusion(f32[32]{0:T(128)S(1)} %bitcast.201, f32[32]{0:T(128)S(1)} %bitcast.202, f32[32,32,128]{2,1,0:T(8,128)S(1)} %add_rsqrt_fusion, f32[32,32,32,128]{3,2,1,0:T(8,128)} %get-tuple-element.36, f32[32,32,128]{2,1,0:T(8,128)S(1)} %broadcast_multiply_fusion), kind=kLoop, calls=%fused_computation.40 | loop fusion | flops 289406976 | bytes 26214656 | tf_op jit(solution)/shard_map/broadcast_in_dim | solution.py:136
  (42 shorter events, 13.5 us)
Async XLA Ops:
  7.4 23.8 %copy-start = (bf16[1,32,32]{2,1,0:T(8,128)(2,1)S(1)}, bf16[1,32,32]{2,1,0:T(8,128)(2,1)}, u32[]{:S(2)}) copy-start(bf16[1,32,32]{2,1,0:T(8,128)(2,1)} %param.8) | copy-start | bytes 6148
  7.4 69.8 %reduce-scatter.3.cloned.1.call-start = ((), (), s32[]{:S(2)}) async-start(), calls=%async_computation.2 | async-start | bytes 5242880 | tf_op jit(solution)/shard_map/reduce_scatter | solution.py:95
  29.7 61.4 %all-gather.3.cloned.1.call-start = ((), (), s32[]{:S(2)}) async-start(), calls=%async_computation.4 | async-start | bytes 6291456 | tf_op jit(solution)/shard_map/all_gather | solution.py:103
  30.3 72.8 %reduce-scatter.5.cloned.1.call-start = ((), (), s32[]{:S(2)}) async-start(), calls=%async_computation.3 | async-start | bytes 655360 | tf_op jit(solution)/shard_map/reduce_scatter | solution.py:99
  120.5 16.0 %collective-permute-start = (bf16[4,16,32,2,16]{2,0,3,4,1:T(4,128)(2,1)S(1)}, bf16[4,16,32,2,16]{2,0,3,4,1:T(4,128)(2,1)S(1)}, u32[]{:S(2)}, u32[]{:S(2)}) collective-permute-start(bf16[4,16,32,2,16]{2,0,3,4,1:T(4,128)(2,1)S(1)} %copy.30), channel_id=1, source_target_pairs={{0,8},{8,16},{16,24},{24,0},{1,9},{9,17},{17,25},{25,1},{2,10},{10... | collective-permute-start | bytes 393224 | tf_op jit(solution)/shard_map/ppermute | solution.py:111
  136.5 15.1 %collective-permute-start.1 = (bf16[4,16,32,2,16]{2,0,3,4,1:T(4,128)(2,1)S(1)}, bf16[4,16,32,2,16]{2,0,3,4,1:T(4,128)(2,1)S(1)}, u32[]{:S(2)}, u32[]{:S(2)}) collective-permute-start(bf16[4,16,32,2,16]{2,0,3,4,1:T(4,128)(2,1)S(1)} %collective-permute-done), channel_id=1, source_target_pairs={{0,8},{8,16},{16,24},{24,0},{1,9},{9,17},{17,25},{25,1},{2,10},{10... | collective-permute-start | bytes 393224 | tf_op jit(solution)/shard_map/ppermute | solution.py:111
  151.7 14.4 %collective-permute-start.2 = (bf16[4,16,32,2,16]{2,0,3,4,1:T(4,128)(2,1)S(1)}, bf16[4,16,32,2,16]{2,0,3,4,1:T(4,128)(2,1)S(1)}, u32[]{:S(2)}, u32[]{:S(2)}) collective-permute-start(bf16[4,16,32,2,16]{2,0,3,4,1:T(4,128)(2,1)S(1)} %collective-permute-done.1), channel_id=1, source_target_pairs={{0,8},{8,16},{16,24},{24,0},{1,9},{9,17},{17,25},{25,1},{2,10},{10... | collective-permute-start | bytes 393224 | tf_op jit(solution)/shard_map/ppermute | solution.py:111
  173.6 33.3 %copy-start.4 = (f32[1,32]{1,0:T(1,128)S(1)}, f32[1,32]{1,0:T(1,128)}, u32[]{:S(2)}) copy-start(f32[1,32]{1,0:T(1,128)} %param.9) | copy-start | bytes 388
  221.4 11.1 %copy-start.2 = (f32[1,32]{1,0:T(1,128)S(1)}, f32[1,32]{1,0:T(1,128)}, u32[]{:S(2)}) copy-start(f32[1,32]{1,0:T(1,128)} %param.11) | copy-start | bytes 388
  221.4 11.1 %copy-start.3 = (f32[1,32]{1,0:T(1,128)S(1)}, f32[1,32]{1,0:T(1,128)}, u32[]{:S(2)}) copy-start(f32[1,32]{1,0:T(1,128)} %param.10) | copy-start | bytes 388
  221.4 52.5 %copy-start.1 = (bf16[1,32,32]{2,1,0:T(8,128)(2,1)S(1)}, bf16[1,32,32]{2,1,0:T(8,128)(2,1)}, u32[]{:S(2)}) copy-start(bf16[1,32,32]{2,1,0:T(8,128)(2,1)} %param.8) | copy-start | bytes 6148
Sparse Core Ops, SparseCore 0:
  29.9 47.2 reduce-scatter.2
  80.2 21.8 reduce-scatter.4
Sparse Core Ops, SparseCore 1:
  31.8 59.3 all-gather.2
